TPU v7x, 128 devices: a whole 4x4x4 slice. The times are simulated.
128 devices in a mesh: section: 8 (over y, core), dp: 16 (over z, x).
Axes of the slice: x: 4, y: 4, z: 4, core: 2. Of those that a mesh axis runs over, the one named last changes fastest.
Arguments:
- acts: bfloat16 [8, 8192, 3584], P('section', 'dp'), may hold values from -400 to 400
- cotangent: bfloat16 [8192, 3584], P('dp'), may hold values from -6 to 6
- frozen: bfloat16 [8, 3584, 3584], P('section', 'dp'), may hold values from -0.09375 to 0.09375
- down_adapter: bfloat16 [8, 16, 3584], P('section'), may hold values from -0.25 to 0.25
- up_adapter: bfloat16 [8, 16, 3584], P('section'), may hold values from -0.25 to 0.25
- example_ids: int32 [16, 4], P('dp'), may hold values from 0 to 3, each once within a row
- lengths: int32 [16, 4], P('dp'), may hold values from 32 to 128
Outputs:
- grad_down: float32 [8, 16, 3584], P('section', None, 'dp')
- grad_up: float32 [8, 16, 3584], P('section', None, 'dp')
- example_norms: float32 [16, 4], P('dp')
Inputs may be any that keep to these rules, and one draw needn't show every extreme that they name: `example_ids`: each row is an ordering of the 4 examples of one replica.
All inputs are finite; a program needn't handle non-finite values.
Results may differ from a plain program's by a relative error of at most 0.009.
Values may be sent and summed in bfloat16 or wider, within the bound.
A program may use at most 128 MiB of HBM per device.

v0:
```python
import math
import jax
import jax.numpy as jnp
from jax import lax
from jax.sharding import PartitionSpec as P


def from_behind(value, axis, steps):
    count = lax.axis_size(axis)
    first, last = (max(0, -steps), min(count, count - steps))
    return lax.ppermute(value, axis, [(source, source + steps) for source in range(first, last)])


def sent_to_all(value, axis):
    size = lax.axis_size(axis)
    return lax.all_to_all(
        jnp.broadcast_to(value[None], (size, *value.shape)), axis, 0, 0, tiled=True
    )


def taken_together(value, axis):
    return sent_to_all(value, axis).sum(axis=0)


def split_up(value, dim, size):
    shape = value.shape
    pieces = value.reshape(*shape[:dim], size, shape[dim] // size, *shape[dim + 1 :])
    return jnp.moveaxis(pieces, dim, 0)


def sent_and_summed(value, axis, dim):
    pieces = split_up(value, dim, lax.axis_size(axis))
    arrived = lax.all_to_all(pieces, axis, split_axis=0, concat_axis=0, tiled=True)
    return arrived.sum(axis=0)


def side_by_side(arrays, axis, dim, along):
    ends, at = ([], 0)
    for a in arrays[:-1]:
        at += a.shape[along]
        ends.append(at)
    both = jnp.concatenate(arrays, axis=along)
    return tuple(jnp.split(sent_and_summed(both, axis, dim), ends, axis=along))


def on_device(acts, cotangent, frozen, down_adapter, up_adapter, example_ids, lengths):
    section_count = lax.axis_size("section")
    section_index = lax.axis_index("section")
    replica_count = lax.axis_size("dp")
    layer_inputs = acts[0]
    down_rows = down_adapter[0]
    up_rows = up_adapter[0]
    slot_count = example_ids.shape[1]
    positions = layer_inputs.shape[0] // slot_count
    features = layer_inputs.shape[1]
    rank_size = down_rows.shape[0]
    choose = (example_ids[0][:, None] == jnp.arange(slot_count, dtype=jnp.int32)[None, :]).astype(
        jnp.int32
    )
    slot_length = jnp.sum(choose * lengths[0][None, :], axis=1)
    live_mask = (jnp.arange(positions, dtype=jnp.int32)[None, :] < slot_length[:, None]).astype(
        jnp.bfloat16
    )
    seeded = cotangent.reshape(slot_count, positions, features) * live_mask[:, :, None]
    input_blocks = layer_inputs.reshape(slot_count, positions, features)
    clip_scale = math.sqrt(2.0 * rank_size * features) / math.sqrt(replica_count * slot_count)
    weight = lax.all_gather(frozen[0], "dp", axis=0, tiled=True)

    def backstep(out_grad):
        up_grad = jnp.dot(out_grad, up_rows.T, preferred_element_type=jnp.float32).astype(
            jnp.bfloat16
        )
        in_grad = jnp.dot(out_grad, weight.T, preferred_element_type=jnp.float32)
        in_grad = in_grad + jnp.dot(up_grad, down_rows, preferred_element_type=jnp.float32)
        return in_grad.astype(jnp.bfloat16)

    def local_terms(out_grad, inputs):
        up_grad = jnp.dot(out_grad, up_rows.T, preferred_element_type=jnp.float32).astype(
            jnp.bfloat16
        )
        down_act = jnp.dot(inputs, down_rows.T, preferred_element_type=jnp.float32).astype(
            jnp.bfloat16
        )
        down_term = jnp.dot(up_grad.T, inputs, preferred_element_type=jnp.float32)
        up_term = jnp.dot(down_act.T, out_grad, preferred_element_type=jnp.float32)
        square_sum = jnp.sum(down_term * down_term) + jnp.sum(up_term * up_term)
        return (square_sum, down_term, up_term)

    tick_count = slot_count + section_count - 1
    incoming = jnp.zeros((positions, features), jnp.bfloat16)
    stored_grads = jnp.zeros((slot_count, positions, features), jnp.bfloat16)
    sum_down = jnp.zeros((rank_size, features), jnp.float32)
    sum_up = jnp.zeros((rank_size, features), jnp.float32)
    slot_norms = jnp.zeros((slot_count,), jnp.float32)

    def tick_step(tick, carry):
        incoming, stored_grads, sum_down, sum_up, slot_norms = carry
        micro_index = tick - (section_count - 1 - section_index)
        active = (micro_index >= 0) & (micro_index < slot_count)
        held_index = jnp.clip(micro_index, 0, slot_count - 1)
        fresh = lax.dynamic_index_in_dim(seeded, held_index, 0, keepdims=False)
        start = jnp.where(section_index == section_count - 1, fresh, incoming)
        produced = lax.cond(active, backstep, lambda value: jnp.zeros_like(value), start)
        previous = lax.dynamic_index_in_dim(stored_grads, held_index, 0, keepdims=False)
        kept = jnp.where(active, start, previous)
        stored_grads = lax.dynamic_update_index_in_dim(stored_grads, kept, held_index, 0)
        incoming = from_behind(produced, "section", -1)
        return (incoming, stored_grads, sum_down, sum_up, slot_norms)

    carry = (incoming, stored_grads, sum_down, sum_up, slot_norms)
    incoming, stored_grads, sum_down, sum_up, slot_norms = lax.fori_loop(
        0, tick_count, tick_step, carry
    )
    square_sums, down_terms, up_terms = jax.vmap(local_terms)(stored_grads, input_blocks)
    totals = taken_together(square_sums, "section")
    slot_norms = jnp.sqrt(totals)
    factors = clip_scale / (slot_norms + 0.01)
    sum_down = jnp.sum(factors[:, None, None] * down_terms, axis=0)
    sum_up = jnp.sum(factors[:, None, None] * up_terms, axis=0)
    grad_down, grad_up = side_by_side((sum_down, sum_up), "dp", 1, 0)
    example_norms = jnp.sum(choose.astype(jnp.float32) * slot_norms[:, None], axis=0)
    return (grad_down[None], grad_up[None], example_norms[None])


def solution(mesh):
    in_specs = (
        P("section", "dp", None),
        P("dp", None),
        P("section", "dp", None),
        P("section", None, None),
        P("section", None, None),
        P("dp", None),
        P("dp", None),
    )
    out_specs = (P("section", None, "dp"), P("section", None, "dp"), P("dp", None))
    return jax.shard_map(
        on_device, mesh=mesh, in_specs=in_specs, out_specs=out_specs, check_vma=False
    )
```

profile of v0, /device:TPU:0, one launch (start us, length us, event | category | flops | bytes accessed | tf_op | source)
XLA Modules:
  0.0 538.0 jit_solution(118021196939126210)
XLA Ops:
  8.8 4.1 broadcast_multiply_fusion
  13.0 156.6 %all-gather.3.cloned.1.call-done = bf16[1,3584,3584]{2,1,0:T(8,128)(2,1)} async-done(((bf16[1,224,3584]{2,1,0:T(8,128)(2,1)}), bf16[1,3584,3584]{2,1,0:T(8,128)(2,1)}) %all-gather.3.cloned.1.call-update) | async-done | bytes 25690128 | tf_op jit(solution)/shard_map/all_gather | solution.py:67
  169.5 2.1 broadcast_in_dim.35
  171.7 317.0 %while.17 = (s32[]{:T(128)}, bf16[128,3584]{1,0:T(8,128)(2,1)S(1)}, bf16[4,128,3584]{2,1,0:T(8,128)(2,1)}, s32[]{:T(128)}, pred[]{:T(512)}, /*index=5*/bf16[4,12...) while((s32[]{:T(128)}, bf16[128,3584]{1,0:T(8,128)(2,1)S(1)}, ...), condition=%wide.region_4.5_spmd, body=%wide.region_1.4_spmd.sunk | while | flops 3319531520 | bytes 42435348 | solution.py:111
  173.0 2.6 bitcast_dynamic-update-slice_fusion.2
  176.6 1.3 collective-permute-start
  177.9 3.3 collective-permute-done
  182.4 2.6 bitcast_dynamic-update-slice_fusion.2
  186.1 1.3 collective-permute-start
  187.4 13.0 %collective-permute-done = bf16[128,3584]{1,0:T(8,128)(2,1)S(1)} collective-permute-done((bf16[128,3584]{1,0:T(8,128)(2,1)}, bf16[128,3584]{1,0:T(8,128)(2,1)S(1)}, u32[]{:S(2)}, u32[]{:S(2)}) %collective-permute-start) | collective-permute-done | bytes 917536 | tf_op jit(solution)/shard_map/while/body/eval_jaxpr/ppermute | solution.py:11
  201.6 2.6 bitcast_dynamic-update-slice_fusion.2
  205.2 1.3 collective-permute-start
  206.5 13.6 %collective-permute-done = bf16[128,3584]{1,0:T(8,128)(2,1)S(1)} collective-permute-done((bf16[128,3584]{1,0:T(8,128)(2,1)}, bf16[128,3584]{1,0:T(8,128)(2,1)S(1)}, u32[]{:S(2)}, u32[]{:S(2)}) %collective-permute-start) | collective-permute-done | bytes 917536 | tf_op jit(solution)/shard_map/while/body/eval_jaxpr/ppermute | solution.py:11
  221.4 2.6 bitcast_dynamic-update-slice_fusion.2
  225.0 1.3 collective-permute-start
  226.3 13.6 %collective-permute-done = bf16[128,3584]{1,0:T(8,128)(2,1)S(1)} collective-permute-done((bf16[128,3584]{1,0:T(8,128)(2,1)}, bf16[128,3584]{1,0:T(8,128)(2,1)S(1)}, u32[]{:S(2)}, u32[]{:S(2)}) %collective-permute-start) | collective-permute-done | bytes 917536 | tf_op jit(solution)/shard_map/while/body/eval_jaxpr/ppermute | solution.py:11
  241.2 2.6 bitcast_dynamic-update-slice_fusion.2
  244.8 1.3 collective-permute-start
  246.1 13.6 %collective-permute-done = bf16[128,3584]{1,0:T(8,128)(2,1)S(1)} collective-permute-done((bf16[128,3584]{1,0:T(8,128)(2,1)}, bf16[128,3584]{1,0:T(8,128)(2,1)S(1)}, u32[]{:S(2)}, u32[]{:S(2)}) %collective-permute-start) | collective-permute-done | bytes 917536 | tf_op jit(solution)/shard_map/while/body/eval_jaxpr/ppermute | solution.py:11
  261.0 2.6 bitcast_dynamic-update-slice_fusion.2
  265.9 13.6 %collective-permute-done = bf16[128,3584]{1,0:T(8,128)(2,1)S(1)} collective-permute-done((bf16[128,3584]{1,0:T(8,128)(2,1)}, bf16[128,3584]{1,0:T(8,128)(2,1)S(1)}, u32[]{:S(2)}, u32[]{:S(2)}) %collective-permute-start) | collective-permute-done | bytes 917536 | tf_op jit(solution)/shard_map/while/body/eval_jaxpr/ppermute | solution.py:11
  280.8 2.6 bitcast_dynamic-update-slice_fusion.2
  285.7 78.1 %collective-permute-done = bf16[128,3584]{1,0:T(8,128)(2,1)S(1)} collective-permute-done((bf16[128,3584]{1,0:T(8,128)(2,1)}, bf16[128,3584]{1,0:T(8,128)(2,1)S(1)}, u32[]{:S(2)}, u32[]{:S(2)}) %collective-permute-start) | collective-permute-done | bytes 917536 | tf_op jit(solution)/shard_map/while/body/eval_jaxpr/ppermute | solution.py:11
  365.0 2.6 bitcast_dynamic-update-slice_fusion.2
  367.6 15.1 %conditional.2 = (bf16[128,3584]{1,0:T(8,128)(2,1)}) conditional(s32[]{:T(128)} %convert_element_type.57, () %tuple.55, (bf16[128,3584]{1,0:T(8,128)(2,1)S(1)}, bf16[3584,3584]{1,0:T(8,128)(2,1)}, bf16[16,3584]{1,0:T(8,128)(2,1)S(1)}, bf16[16,3584]{1,0:T(8,128)(2,1)S(1)}) %tuple.56), branch_computations={%region_2.2_spmd, %region_3.3_spmd} | conditional | flops 3318614016 | bytes 32342024 | solution.py:103
  367.6 12.9 %fusion.13 = f32[128,3584]{1,0:T(8,128)S(1)} fusion(bf16[128,3584]{1,0:T(8,128)(2,1)S(1)} %get-tuple-element.202, bf16[3584,3584]{1,0:T(8,128)(2,1)} %get-tuple-element.203), kind=kOutput, calls=%fused_computation.28 | convolution fusion | flops 3288334336 | bytes 28442624 | tf_op jit(solution)/shard_map/while/body/eval_jaxpr/cond/branch_1_fun/dot_general | solution.py:73
  380.5 2.2 fusion
  384.0 13.6 %collective-permute-done = bf16[128,3584]{1,0:T(8,128)(2,1)S(1)} collective-permute-done((bf16[128,3584]{1,0:T(8,128)(2,1)}, bf16[128,3584]{1,0:T(8,128)(2,1)S(1)}, u32[]{:S(2)}, u32[]{:S(2)}) %collective-permute-start) | collective-permute-done | bytes 917536 | tf_op jit(solution)/shard_map/while/body/eval_jaxpr/ppermute | solution.py:11
  398.8 2.6 bitcast_dynamic-update-slice_fusion.2
  401.4 15.1 %conditional.2 = (bf16[128,3584]{1,0:T(8,128)(2,1)}) conditional(s32[]{:T(128)} %convert_element_type.57, () %tuple.55, (bf16[128,3584]{1,0:T(8,128)(2,1)S(1)}, bf16[3584,3584]{1,0:T(8,128)(2,1)}, bf16[16,3584]{1,0:T(8,128)(2,1)S(1)}, bf16[16,3584]{1,0:T(8,128)(2,1)S(1)}) %tuple.56), branch_computations={%region_2.2_spmd, %region_3.3_spmd} | conditional | flops 3318614016 | bytes 32342024 | solution.py:103
  401.4 12.9 %fusion.13 = f32[128,3584]{1,0:T(8,128)S(1)} fusion(bf16[128,3584]{1,0:T(8,128)(2,1)S(1)} %get-tuple-element.202, bf16[3584,3584]{1,0:T(8,128)(2,1)} %get-tuple-element.203), kind=kOutput, calls=%fused_computation.28 | convolution fusion | flops 3288334336 | bytes 28442624 | tf_op jit(solution)/shard_map/while/body/eval_jaxpr/cond/branch_1_fun/dot_general | solution.py:73
  414.3 2.2 fusion
  417.8 13.6 %collective-permute-done = bf16[128,3584]{1,0:T(8,128)(2,1)S(1)} collective-permute-done((bf16[128,3584]{1,0:T(8,128)(2,1)}, bf16[128,3584]{1,0:T(8,128)(2,1)S(1)}, u32[]{:S(2)}, u32[]{:S(2)}) %collective-permute-start) | collective-permute-done | bytes 917536 | tf_op jit(solution)/shard_map/while/body/eval_jaxpr/ppermute | solution.py:11
  432.6 2.6 bitcast_dynamic-update-slice_fusion.2
  435.2 15.1 %conditional.2 = (bf16[128,3584]{1,0:T(8,128)(2,1)}) conditional(s32[]{:T(128)} %convert_element_type.57, () %tuple.55, (bf16[128,3584]{1,0:T(8,128)(2,1)S(1)}, bf16[3584,3584]{1,0:T(8,128)(2,1)}, bf16[16,3584]{1,0:T(8,128)(2,1)S(1)}, bf16[16,3584]{1,0:T(8,128)(2,1)S(1)}) %tuple.56), branch_computations={%region_2.2_spmd, %region_3.3_spmd} | conditional | flops 3318614016 | bytes 32342024 | solution.py:103
  435.2 12.9 %fusion.13 = f32[128,3584]{1,0:T(8,128)S(1)} fusion(bf16[128,3584]{1,0:T(8,128)(2,1)S(1)} %get-tuple-element.202, bf16[3584,3584]{1,0:T(8,128)(2,1)} %get-tuple-element.203), kind=kOutput, calls=%fused_computation.28 | convolution fusion | flops 3288334336 | bytes 28442624 | tf_op jit(solution)/shard_map/while/body/eval_jaxpr/cond/branch_1_fun/dot_general | solution.py:73
  448.1 2.2 fusion
  451.6 13.6 %collective-permute-done = bf16[128,3584]{1,0:T(8,128)(2,1)S(1)} collective-permute-done((bf16[128,3584]{1,0:T(8,128)(2,1)}, bf16[128,3584]{1,0:T(8,128)(2,1)S(1)}, u32[]{:S(2)}, u32[]{:S(2)}) %collective-permute-start) | collective-permute-done | bytes 917536 | tf_op jit(solution)/shard_map/while/body/eval_jaxpr/ppermute | solution.py:11
  466.4 2.6 bitcast_dynamic-update-slice_fusion.2
  469.0 15.1 %conditional.2 = (bf16[128,3584]{1,0:T(8,128)(2,1)}) conditional(s32[]{:T(128)} %convert_element_type.57, () %tuple.55, (bf16[128,3584]{1,0:T(8,128)(2,1)S(1)}, bf16[3584,3584]{1,0:T(8,128)(2,1)}, bf16[16,3584]{1,0:T(8,128)(2,1)S(1)}, bf16[16,3584]{1,0:T(8,128)(2,1)S(1)}) %tuple.56), branch_computations={%region_2.2_spmd, %region_3.3_spmd} | conditional | flops 3318614016 | bytes 32342024 | solution.py:103
  469.0 12.9 %fusion.13 = f32[128,3584]{1,0:T(8,128)S(1)} fusion(bf16[128,3584]{1,0:T(8,128)(2,1)S(1)} %get-tuple-element.202, bf16[3584,3584]{1,0:T(8,128)(2,1)} %get-tuple-element.203), kind=kOutput, calls=%fused_computation.28 | convolution fusion | flops 3288334336 | bytes 28442624 | tf_op jit(solution)/shard_map/while/body/eval_jaxpr/cond/branch_1_fun/dot_general | solution.py:73
  481.9 2.2 fusion
  485.4 3.3 collective-permute-done
  488.7 4.9 multiply_reduce_fusion.3
  493.6 4.9 multiply_reduce_fusion.2
  498.5 13.5 %all_to_all.11 = f32[8,1,4]{2,1,0:T(1,128)S(1)} all-to-all(f32[8,1,4]{2,1,0:T(1,128)S(1)} %broadcast_in_dim.36), channel_id=1, replica_groups=mesh['section'=8,'dp'=16] {'section'}, dimensions={0} | all-to-all | bytes 256 | tf_op jit(solution)/shard_map/all_to_all | solution.py:16
  513.7 5.3 all-to-all-start.1
  519.6 10.9 %all-to-all-done.1 = f32[16,32,224]{2,1,0:T(8,128)S(1)} async-done(((f32[16,32,224]{2,1,0:T(8,128)}), f32[16,32,224]{2,1,0:T(8,128)S(1)}, u32[]{:S(2)}, u32[]{:S(2)}) %all-to-all-start.1) | async-done | bytes 458784 | tf_op jit(solution)/shard_map/all_to_all | solution.py:33
  (53 shorter events, 40.3 us)
Async XLA Ops:
  7.2 162.4 %all-gather.3.cloned.1.call-start = ((), (), s32[]{:S(2)}) async-start(), calls=%async_computation.2 | async-start | bytes 27295744 | tf_op jit(solution)/shard_map/all_gather | solution.py:67
  13.0 158.7 %copy-start = (bf16[1,16,3584]{2,1,0:T(8,128)(2,1)S(1)}, bf16[1,16,3584]{2,1,0:T(8,128)(2,1)}, u32[]{:S(2)}) copy-start(bf16[1,16,3584]{2,1,0:T(8,128)(2,1)} %param.15) | copy-start | bytes 344068
  13.0 158.7 %copy-start.1 = (bf16[1,16,3584]{2,1,0:T(8,128)(2,1)S(1)}, bf16[1,16,3584]{2,1,0:T(8,128)(2,1)}, u32[]{:S(2)}) copy-start(bf16[1,16,3584]{2,1,0:T(8,128)(2,1)} %param.14) | copy-start | bytes 344068
  176.6 4.6 collective-permute-start
  186.1 14.3 %collective-permute-start = (bf16[128,3584]{1,0:T(8,128)(2,1)}, bf16[128,3584]{1,0:T(8,128)(2,1)S(1)}, u32[]{:S(2)}, u32[]{:S(2)}) collective-permute-start(bf16[128,3584]{1,0:T(8,128)(2,1)} %get-tuple-element.349), channel_id=1, source_target_pairs={{16,0},{32,16},{48,32},{64,48},{80,64},{96,80},{112,96},{17,1},{33... | collective-permute-start | bytes 2752520 | tf_op jit(solution)/shard_map/while/body/eval_jaxpr/ppermute | solution.py:11
  205.2 14.9 %collective-permute-start = (bf16[128,3584]{1,0:T(8,128)(2,1)}, bf16[128,3584]{1,0:T(8,128)(2,1)S(1)}, u32[]{:S(2)}, u32[]{:S(2)}) collective-permute-start(bf16[128,3584]{1,0:T(8,128)(2,1)} %get-tuple-element.349), channel_id=1, source_target_pairs={{16,0},{32,16},{48,32},{64,48},{80,64},{96,80},{112,96},{17,1},{33... | collective-permute-start | bytes 2752520 | tf_op jit(solution)/shard_map/while/body/eval_jaxpr/ppermute | solution.py:11
  225.0 14.9 %collective-permute-start = (bf16[128,3584]{1,0:T(8,128)(2,1)}, bf16[128,3584]{1,0:T(8,128)(2,1)S(1)}, u32[]{:S(2)}, u32[]{:S(2)}) collective-permute-start(bf16[128,3584]{1,0:T(8,128)(2,1)} %get-tuple-element.349), channel_id=1, source_target_pairs={{16,0},{32,16},{48,32},{64,48},{80,64},{96,80},{112,96},{17,1},{33... | collective-permute-start | bytes 2752520 | tf_op jit(solution)/shard_map/while/body/eval_jaxpr/ppermute | solution.py:11
  244.8 14.9 %collective-permute-start = (bf16[128,3584]{1,0:T(8,128)(2,1)}, bf16[128,3584]{1,0:T(8,128)(2,1)S(1)}, u32[]{:S(2)}, u32[]{:S(2)}) collective-permute-start(bf16[128,3584]{1,0:T(8,128)(2,1)} %get-tuple-element.349), channel_id=1, source_target_pairs={{16,0},{32,16},{48,32},{64,48},{80,64},{96,80},{112,96},{17,1},{33... | collective-permute-start | bytes 2752520 | tf_op jit(solution)/shard_map/while/body/eval_jaxpr/ppermute | solution.py:11
  264.6 14.9 %collective-permute-start = (bf16[128,3584]{1,0:T(8,128)(2,1)}, bf16[128,3584]{1,0:T(8,128)(2,1)S(1)}, u32[]{:S(2)}, u32[]{:S(2)}) collective-permute-start(bf16[128,3584]{1,0:T(8,128)(2,1)} %get-tuple-element.349), channel_id=1, source_target_pairs={{16,0},{32,16},{48,32},{64,48},{80,64},{96,80},{112,96},{17,1},{33... | collective-permute-start | bytes 2752520 | tf_op jit(solution)/shard_map/while/body/eval_jaxpr/ppermute | solution.py:11
  284.4 79.4 %collective-permute-start = (bf16[128,3584]{1,0:T(8,128)(2,1)}, bf16[128,3584]{1,0:T(8,128)(2,1)S(1)}, u32[]{:S(2)}, u32[]{:S(2)}) collective-permute-start(bf16[128,3584]{1,0:T(8,128)(2,1)} %get-tuple-element.349), channel_id=1, source_target_pairs={{16,0},{32,16},{48,32},{64,48},{80,64},{96,80},{112,96},{17,1},{33... | collective-permute-start | bytes 2752520 | tf_op jit(solution)/shard_map/while/body/eval_jaxpr/ppermute | solution.py:11
  382.7 14.9 %collective-permute-start = (bf16[128,3584]{1,0:T(8,128)(2,1)}, bf16[128,3584]{1,0:T(8,128)(2,1)S(1)}, u32[]{:S(2)}, u32[]{:S(2)}) collective-permute-start(bf16[128,3584]{1,0:T(8,128)(2,1)} %get-tuple-element.349), channel_id=1, source_target_pairs={{16,0},{32,16},{48,32},{64,48},{80,64},{96,80},{112,96},{17,1},{33... | collective-permute-start | bytes 2752520 | tf_op jit(solution)/shard_map/while/body/eval_jaxpr/ppermute | solution.py:11
  416.5 14.9 %collective-permute-start = (bf16[128,3584]{1,0:T(8,128)(2,1)}, bf16[128,3584]{1,0:T(8,128)(2,1)S(1)}, u32[]{:S(2)}, u32[]{:S(2)}) collective-permute-start(bf16[128,3584]{1,0:T(8,128)(2,1)} %get-tuple-element.349), channel_id=1, source_target_pairs={{16,0},{32,16},{48,32},{64,48},{80,64},{96,80},{112,96},{17,1},{33... | collective-permute-start | bytes 2752520 | tf_op jit(solution)/shard_map/while/body/eval_jaxpr/ppermute | solution.py:11
  450.3 14.9 %collective-permute-start = (bf16[128,3584]{1,0:T(8,128)(2,1)}, bf16[128,3584]{1,0:T(8,128)(2,1)S(1)}, u32[]{:S(2)}, u32[]{:S(2)}) collective-permute-start(bf16[128,3584]{1,0:T(8,128)(2,1)} %get-tuple-element.349), channel_id=1, source_target_pairs={{16,0},{32,16},{48,32},{64,48},{80,64},{96,80},{112,96},{17,1},{33... | collective-permute-start | bytes 2752520 | tf_op jit(solution)/shard_map/while/body/eval_jaxpr/ppermute | solution.py:11
  484.1 4.6 collective-permute-start
  498.4 20.5 %copy-start.2 = (s32[1,4]{1,0:T(1,128)S(1)}, s32[1,4]{1,0:T(1,128)}, u32[]{:S(2)}) copy-start(s32[1,4]{1,0:T(1,128)} %param.16) | copy-start | bytes 52
  513.7 16.8 %all-to-all-start.1 = ((f32[16,32,224]{2,1,0:T(8,128)}), f32[16,32,224]{2,1,0:T(8,128)S(1)}, u32[]{:S(2)}, u32[]{:S(2)}) async-start(f32[16,32,224]{2,1,0:T(8,128)} %copy.13), calls=%async_computation.1 | async-start | bytes 1048576 | tf_op jit(solution)/shard_map/all_to_all | solution.py:33
Sparse Core Ops, SparseCore 0:
  10.1 159.3 all-gather.2
where the time goes:
time: 539 us; the launch traced here: 538 us
  waiting for transfers between devices  361 us (67%)
  matrix products  70.1 us (13%)
  other arithmetic  34.6 us (6%)
  local copies, waits for them, and re-layouts  25 us (5%)
  starting transfers between devices  19.4 us (4%)
  between operations  14.1 us (3%)
  blocking collectives  13.5 us (3%)
    ppermute x11, waiting for transfers between devices, from_behind(): lax.ppermute(value, axis, [(source, source + steps) for source in range(f...  193 us
    all_gather x1, waiting for transfers between devices, on_device(): weight = lax.all_gather(frozen[0], 'dp', axis=0, tiled=True)  157 us
    dot_general x4, matrix products, backstep(): in_grad = jnp.dot(out_grad, weight.T, preferred_element_type=jnp.float32)  51.6 us
    dynamic_update_slice x11, other arithmetic, tick_step(): lax.dynamic_update_index_in_dim(stored_grads, kept, held_index, 0)  28.6 us
    ppermute x11, starting transfers between devices, from_behind(): lax.ppermute(value, axis, [(source, source + steps) for source in range(f...  14.1 us
    dynamic_slice x11, local copies, waits for them, and re-layouts, tick_step(): lax.dynamic_index_in_dim(stored_grads, held_index, 0, keepdims=False)  13.6 us
    all_to_all x1, blocking collectives, sent_to_all(): lax.all_to_all(jnp.broadcast_to(value[None], (size, *value.shape)), axis,...  13.5 us
    all_to_all x1, waiting for transfers between devices, sent_and_summed(): lax.all_to_all(pieces, axis, split_axis=0, concat_axis=0, tiled=True)  10.9 us
  transfers between devices with their start and end apart: 13, of which 13 were waited for; matrix products, arithmetic and copies ran while one was open for 1% of the time, Pallas kernels for 0%

commit v1 on v0

--- a/solution.py
+++ b/solution.py
@@ -64,7 +64,9 @@
     seeded = cotangent.reshape(slot_count, positions, features) * live_mask[:, :, None]
     input_blocks = layer_inputs.reshape(slot_count, positions, features)
     clip_scale = math.sqrt(2.0 * rank_size * features) / math.sqrt(replica_count * slot_count)
-    weight = lax.all_gather(frozen[0], "dp", axis=0, tiled=True)
+    own = frozen[0]
+    sent = jnp.stack([own] * lax.axis_size("dp"))
+    weight = jnp.concatenate(lax.all_to_all(sent, "dp", 0, 0), axis=0)
 
     def backstep(out_grad):
         up_grad = jnp.dot(out_grad, up_rows.T, preferred_element_type=jnp.float32).astype(

time: 539 us -> 764 us (1.42)
  waiting for transfers between devices: 361 us -> 583 us
  between operations: 14.1 us -> 0.73 us
  local copies, waits for them, and re-layouts: 25 us -> 34.8 us
    all_to_all x0 -> x1, waiting for transfers between devices: none -> 379 us  [on_device(): weight = jnp.concatenate(lax.all_to_all(sent, 'dp', 0, 0), axis=0)]
    all_gather x1 -> x0, waiting for transfers between devices: 157 us -> none  [on_device(): weight = lax.all_gather(frozen[0], 'dp', axis=0, tiled=True)]
    another operation x8 -> x9, local copies, waits for them, and re-layouts: 7.19 us -> 17 us  [the longest x1 9.6 us: on_device(): sent = jnp.stack([own] * lax.axis_size('dp'))]
    all_to_all x0 -> x1, starting transfers between devices: none -> 8.18 us  [on_device(): weight = jnp.concatenate(lax.all_to_all(sent, 'dp', 0, 0), axis=0)]
where the time goes in v1:
time: 764 us; the launch traced here: 762 us
  waiting for transfers between devices  583 us (76%)
  matrix products  70.2 us (9%)
  local copies, waits for them, and re-layouts  34.8 us (5%)
  other arithmetic  34.1 us (4%)
  starting transfers between devices  25.8 us (3%)
  blocking collectives  13.5 us (2%)
    all_to_all x1, waiting for transfers between devices, on_device(): weight = jnp.concatenate(lax.all_to_all(sent, 'dp', 0, 0), axis=0)  379 us
    ppermute x11, waiting for transfers between devices, from_behind(): lax.ppermute(value, axis, [(source, source + steps) for source in range(f...  192 us
    dot_general x4, matrix products, backstep(): in_grad = jnp.dot(out_grad, weight.T, preferred_element_type=jnp.float32)  51.6 us
    dynamic_update_slice x11, other arithmetic, tick_step(): lax.dynamic_update_index_in_dim(stored_grads, kept, held_index, 0)  28.7 us
  transfers between devices with their start and end apart: 13, of which 13 were waited for; matrix products, arithmetic and copies ran while one was open for 1% of the time, Pallas kernels for 0%

profile of v1, /device:TPU:0, one launch (start us, length us, event | category | flops | bytes accessed | tf_op | source)
XLA Modules:
  0.0 762.1 jit_solution(15620111590895417232)
XLA Ops:
  0.6 9.6 %stack.3 = bf16[16,224,3584]{2,1,0:T(8,128)(2,1)} broadcast(bf16[224,3584]{1,0:T(8,128)(2,1)} %bitcast.56), dimensions={1,2} | broadcast | bytes 27295744 | tf_op jit(solution)/shard_map/stack | solution.py:68
  10.2 8.2 %all-to-all-start = ((bf16[16,224,3584]{2,1,0:T(8,128)(2,1)}), bf16[16,224,3584]{2,1,0:T(8,128)(2,1)}, u32[]{:S(2)}, u32[]{:S(2)}) async-start(bf16[16,224,3584]{2,1,0:T(8,128)(2,1)} %stack.3), calls=%async_computation | async-start | bytes 51380224 | tf_op jit(solution)/shard_map/all_to_all | solution.py:69
  18.7 4.2 broadcast_multiply_fusion
  23.0 379.3 %all-to-all-done = bf16[16,224,3584]{2,1,0:T(8,128)(2,1)} async-done(((bf16[16,224,3584]{2,1,0:T(8,128)(2,1)}), bf16[16,224,3584]{2,1,0:T(8,128)(2,1)}, u32[]{:S(2)}, u32[]{:S(2)}) %all-to-all-start) | async-done | bytes 25690144 | tf_op jit(solution)/shard_map/all_to_all | solution.py:69
  402.3 2.1 broadcast_in_dim.35
  404.4 316.7 %while.17 = (s32[]{:T(128)}, bf16[128,3584]{1,0:T(8,128)(2,1)S(1)}, bf16[4,128,3584]{2,1,0:T(8,128)(2,1)}, s32[]{:T(128)}, pred[]{:T(512)}, /*index=5*/bf16[4,12...) while((s32[]{:T(128)}, bf16[128,3584]{1,0:T(8,128)(2,1)S(1)}, ...), condition=%wide.region_4.5_spmd, body=%wide.region_1.4_spmd.sunk | while | flops 3319531520 | bytes 42435348 | solution.py:113
  405.7 2.6 bitcast_dynamic-update-slice_fusion.2
  409.4 1.3 collective-permute-start
  410.7 3.3 collective-permute-done
  415.2 2.6 bitcast_dynamic-update-slice_fusion.2
  418.8 1.3 collective-permute-start
  420.1 13.1 %collective-permute-done = bf16[128,3584]{1,0:T(8,128)(2,1)S(1)} collective-permute-done((bf16[128,3584]{1,0:T(8,128)(2,1)}, bf16[128,3584]{1,0:T(8,128)(2,1)S(1)}, u32[]{:S(2)}, u32[]{:S(2)}) %collective-permute-start) | collective-permute-done | bytes 917536 | tf_op jit(solution)/shard_map/while/body/eval_jaxpr/ppermute | solution.py:11
  434.5 2.6 bitcast_dynamic-update-slice_fusion.2
  438.1 1.3 collective-permute-start
  439.4 13.6 %collective-permute-done = bf16[128,3584]{1,0:T(8,128)(2,1)S(1)} collective-permute-done((bf16[128,3584]{1,0:T(8,128)(2,1)}, bf16[128,3584]{1,0:T(8,128)(2,1)S(1)}, u32[]{:S(2)}, u32[]{:S(2)}) %collective-permute-start) | collective-permute-done | bytes 917536 | tf_op jit(solution)/shard_map/while/body/eval_jaxpr/ppermute | solution.py:11
  454.3 2.6 bitcast_dynamic-update-slice_fusion.2
  459.3 13.6 %collective-permute-done = bf16[128,3584]{1,0:T(8,128)(2,1)S(1)} collective-permute-done((bf16[128,3584]{1,0:T(8,128)(2,1)}, bf16[128,3584]{1,0:T(8,128)(2,1)S(1)}, u32[]{:S(2)}, u32[]{:S(2)}) %collective-permute-start) | collective-permute-done | bytes 917536 | tf_op jit(solution)/shard_map/while/body/eval_jaxpr/ppermute | solution.py:11
  474.1 2.6 bitcast_dynamic-update-slice_fusion.2
  479.1 13.6 %collective-permute-done = bf16[128,3584]{1,0:T(8,128)(2,1)S(1)} collective-permute-done((bf16[128,3584]{1,0:T(8,128)(2,1)}, bf16[128,3584]{1,0:T(8,128)(2,1)S(1)}, u32[]{:S(2)}, u32[]{:S(2)}) %collective-permute-start) | collective-permute-done | bytes 917536 | tf_op jit(solution)/shard_map/while/body/eval_jaxpr/ppermute | solution.py:11
  494.0 2.6 bitcast_dynamic-update-slice_fusion.2
  498.9 13.6 %collective-permute-done = bf16[128,3584]{1,0:T(8,128)(2,1)S(1)} collective-permute-done((bf16[128,3584]{1,0:T(8,128)(2,1)}, bf16[128,3584]{1,0:T(8,128)(2,1)S(1)}, u32[]{:S(2)}, u32[]{:S(2)}) %collective-permute-start) | collective-permute-done | bytes 917536 | tf_op jit(solution)/shard_map/while/body/eval_jaxpr/ppermute | solution.py:11
  513.8 2.6 bitcast_dynamic-update-slice_fusion.2
  518.8 77.3 %collective-permute-done = bf16[128,3584]{1,0:T(8,128)(2,1)S(1)} collective-permute-done((bf16[128,3584]{1,0:T(8,128)(2,1)}, bf16[128,3584]{1,0:T(8,128)(2,1)S(1)}, u32[]{:S(2)}, u32[]{:S(2)}) %collective-permute-start) | collective-permute-done | bytes 917536 | tf_op jit(solution)/shard_map/while/body/eval_jaxpr/ppermute | solution.py:11
  597.3 2.6 bitcast_dynamic-update-slice_fusion.2
  599.9 15.1 %conditional.2 = (bf16[128,3584]{1,0:T(8,128)(2,1)}) conditional(s32[]{:T(128)} %convert_element_type.57, () %tuple.55, (bf16[128,3584]{1,0:T(8,128)(2,1)S(1)}, bf16[3584,3584]{1,0:T(8,128)(2,1)}, bf16[16,3584]{1,0:T(8,128)(2,1)S(1)}, bf16[16,3584]{1,0:T(8,128)(2,1)S(1)}) %tuple.56), branch_computations={%region_2.2_spmd, %region_3.3_spmd} | conditional | flops 3318614016 | bytes 32342024 | solution.py:105
  599.9 12.9 %fusion.13 = f32[128,3584]{1,0:T(8,128)S(1)} fusion(bf16[128,3584]{1,0:T(8,128)(2,1)S(1)} %get-tuple-element.202, bf16[3584,3584]{1,0:T(8,128)(2,1)} %get-tuple-element.203), kind=kOutput, calls=%fused_computation.28 | convolution fusion | flops 3288334336 | bytes 28442624 | tf_op jit(solution)/shard_map/while/body/eval_jaxpr/cond/branch_1_fun/dot_general | solution.py:75
  612.8 2.2 fusion
  616.4 13.6 %collective-permute-done = bf16[128,3584]{1,0:T(8,128)(2,1)S(1)} collective-permute-done((bf16[128,3584]{1,0:T(8,128)(2,1)}, bf16[128,3584]{1,0:T(8,128)(2,1)S(1)}, u32[]{:S(2)}, u32[]{:S(2)}) %collective-permute-start) | collective-permute-done | bytes 917536 | tf_op jit(solution)/shard_map/while/body/eval_jaxpr/ppermute | solution.py:11
  631.1 2.6 bitcast_dynamic-update-slice_fusion.2
  633.7 15.1 %conditional.2 = (bf16[128,3584]{1,0:T(8,128)(2,1)}) conditional(s32[]{:T(128)} %convert_element_type.57, () %tuple.55, (bf16[128,3584]{1,0:T(8,128)(2,1)S(1)}, bf16[3584,3584]{1,0:T(8,128)(2,1)}, bf16[16,3584]{1,0:T(8,128)(2,1)S(1)}, bf16[16,3584]{1,0:T(8,128)(2,1)S(1)}) %tuple.56), branch_computations={%region_2.2_spmd, %region_3.3_spmd} | conditional | flops 3318614016 | bytes 32342024 | solution.py:105
  633.7 12.9 %fusion.13 = f32[128,3584]{1,0:T(8,128)S(1)} fusion(bf16[128,3584]{1,0:T(8,128)(2,1)S(1)} %get-tuple-element.202, bf16[3584,3584]{1,0:T(8,128)(2,1)} %get-tuple-element.203), kind=kOutput, calls=%fused_computation.28 | convolution fusion | flops 3288334336 | bytes 28442624 | tf_op jit(solution)/shard_map/while/body/eval_jaxpr/cond/branch_1_fun/dot_general | solution.py:75
  646.6 2.2 fusion
  650.1 13.6 %collective-permute-done = bf16[128,3584]{1,0:T(8,128)(2,1)S(1)} collective-permute-done((bf16[128,3584]{1,0:T(8,128)(2,1)}, bf16[128,3584]{1,0:T(8,128)(2,1)S(1)}, u32[]{:S(2)}, u32[]{:S(2)}) %collective-permute-start) | collective-permute-done | bytes 917536 | tf_op jit(solution)/shard_map/while/body/eval_jaxpr/ppermute | solution.py:11
  665.0 2.6 bitcast_dynamic-update-slice_fusion.2
  667.6 15.1 %conditional.2 = (bf16[128,3584]{1,0:T(8,128)(2,1)}) conditional(s32[]{:T(128)} %convert_element_type.57, () %tuple.55, (bf16[128,3584]{1,0:T(8,128)(2,1)S(1)}, bf16[3584,3584]{1,0:T(8,128)(2,1)}, bf16[16,3584]{1,0:T(8,128)(2,1)S(1)}, bf16[16,3584]{1,0:T(8,128)(2,1)S(1)}) %tuple.56), branch_computations={%region_2.2_spmd, %region_3.3_spmd} | conditional | flops 3318614016 | bytes 32342024 | solution.py:105
  667.6 12.9 %fusion.13 = f32[128,3584]{1,0:T(8,128)S(1)} fusion(bf16[128,3584]{1,0:T(8,128)(2,1)S(1)} %get-tuple-element.202, bf16[3584,3584]{1,0:T(8,128)(2,1)} %get-tuple-element.203), kind=kOutput, calls=%fused_computation.28 | convolution fusion | flops 3288334336 | bytes 28442624 | tf_op jit(solution)/shard_map/while/body/eval_jaxpr/cond/branch_1_fun/dot_general | solution.py:75
  680.5 2.2 fusion
  684.0 13.6 %collective-permute-done = bf16[128,3584]{1,0:T(8,128)(2,1)S(1)} collective-permute-done((bf16[128,3584]{1,0:T(8,128)(2,1)}, bf16[128,3584]{1,0:T(8,128)(2,1)S(1)}, u32[]{:S(2)}, u32[]{:S(2)}) %collective-permute-start) | collective-permute-done | bytes 917536 | tf_op jit(solution)/shard_map/while/body/eval_jaxpr/ppermute | solution.py:11
  698.8 2.6 bitcast_dynamic-update-slice_fusion.2
  701.4 15.1 %conditional.2 = (bf16[128,3584]{1,0:T(8,128)(2,1)}) conditional(s32[]{:T(128)} %convert_element_type.57, () %tuple.55, (bf16[128,3584]{1,0:T(8,128)(2,1)S(1)}, bf16[3584,3584]{1,0:T(8,128)(2,1)}, bf16[16,3584]{1,0:T(8,128)(2,1)S(1)}, bf16[16,3584]{1,0:T(8,128)(2,1)S(1)}) %tuple.56), branch_computations={%region_2.2_spmd, %region_3.3_spmd} | conditional | flops 3318614016 | bytes 32342024 | solution.py:105
  701.4 12.9 %fusion.13 = f32[128,3584]{1,0:T(8,128)S(1)} fusion(bf16[128,3584]{1,0:T(8,128)(2,1)S(1)} %get-tuple-element.202, bf16[3584,3584]{1,0:T(8,128)(2,1)} %get-tuple-element.203), kind=kOutput, calls=%fused_computation.28 | convolution fusion | flops 3288334336 | bytes 28442624 | tf_op jit(solution)/shard_map/while/body/eval_jaxpr/cond/branch_1_fun/dot_general | solution.py:75
  714.3 2.2 fusion
  717.8 3.3 collective-permute-done
  721.1 4.9 multiply_reduce_fusion.3
  726.0 4.9 multiply_reduce_fusion.2
  730.9 13.5 %all_to_all.16 = f32[8,1,4]{2,1,0:T(1,128)S(1)} all-to-all(f32[8,1,4]{2,1,0:T(1,128)S(1)} %broadcast_in_dim.36), channel_id=1, replica_groups=mesh['section'=8,'dp'=16] {'section'}, dimensions={0} | all-to-all | bytes 256 | tf_op jit(solution)/shard_map/all_to_all | solution.py:16
  746.1 3.6 all-to-all-start.2
  750.3 11.2 %all-to-all-done.2 = f32[16,32,224]{2,1,0:T(8,128)S(1)} async-done(((f32[16,32,224]{2,1,0:T(8,128)}), f32[16,32,224]{2,1,0:T(8,128)S(1)}, u32[]{:S(2)}, u32[]{:S(2)}) %all-to-all-start.2) | async-done | bytes 458784 | tf_op jit(solution)/shard_map/all_to_all | solution.py:33
  (55 shorter events, 41.9 us)
Async XLA Ops:
  10.2 8.2 %copy-start.2 = (s32[1,4]{1,0:T(1,128)S(1)}, s32[1,4]{1,0:T(1,128)}, u32[]{:S(2)}) copy-start(s32[1,4]{1,0:T(1,128)} %param.17) | copy-start | bytes 52
  10.2 8.2 %copy-start.3 = (s32[1,4]{1,0:T(1,128)S(1)}, s32[1,4]{1,0:T(1,128)}, u32[]{:S(2)}) copy-start(s32[1,4]{1,0:T(1,128)} %param.16) | copy-start | bytes 52
  10.2 392.0 %all-to-all-start = ((bf16[16,224,3584]{2,1,0:T(8,128)(2,1)}), bf16[16,224,3584]{2,1,0:T(8,128)(2,1)}, u32[]{:S(2)}, u32[]{:S(2)}) async-start(bf16[16,224,3584]{2,1,0:T(8,128)(2,1)} %stack.3), calls=%async_computation | async-start | bytes 51380224 | tf_op jit(solution)/shard_map/all_to_all | solution.py:69
  23.0 381.4 %copy-start = (bf16[1,16,3584]{2,1,0:T(8,128)(2,1)S(1)}, bf16[1,16,3584]{2,1,0:T(8,128)(2,1)}, u32[]{:S(2)}) copy-start(bf16[1,16,3584]{2,1,0:T(8,128)(2,1)} %param.15) | copy-start | bytes 344068
  23.0 381.4 %copy-start.1 = (bf16[1,16,3584]{2,1,0:T(8,128)(2,1)S(1)}, bf16[1,16,3584]{2,1,0:T(8,128)(2,1)}, u32[]{:S(2)}) copy-start(bf16[1,16,3584]{2,1,0:T(8,128)(2,1)} %param.14) | copy-start | bytes 344068
  409.4 4.6 collective-permute-start
  418.8 14.4 %collective-permute-start = (bf16[128,3584]{1,0:T(8,128)(2,1)}, bf16[128,3584]{1,0:T(8,128)(2,1)S(1)}, u32[]{:S(2)}, u32[]{:S(2)}) collective-permute-start(bf16[128,3584]{1,0:T(8,128)(2,1)} %get-tuple-element.349), channel_id=1, source_target_pairs={{16,0},{32,16},{48,32},{64,48},{80,64},{96,80},{112,96},{17,1},{33... | collective-permute-start | bytes 2752520 | tf_op jit(solution)/shard_map/while/body/eval_jaxpr/ppermute | solution.py:11
  438.1 14.9 %collective-permute-start = (bf16[128,3584]{1,0:T(8,128)(2,1)}, bf16[128,3584]{1,0:T(8,128)(2,1)S(1)}, u32[]{:S(2)}, u32[]{:S(2)}) collective-permute-start(bf16[128,3584]{1,0:T(8,128)(2,1)} %get-tuple-element.349), channel_id=1, source_target_pairs={{16,0},{32,16},{48,32},{64,48},{80,64},{96,80},{112,96},{17,1},{33... | collective-permute-start | bytes 2752520 | tf_op jit(solution)/shard_map/while/body/eval_jaxpr/ppermute | solution.py:11
  458.0 14.9 %collective-permute-start = (bf16[128,3584]{1,0:T(8,128)(2,1)}, bf16[128,3584]{1,0:T(8,128)(2,1)S(1)}, u32[]{:S(2)}, u32[]{:S(2)}) collective-permute-start(bf16[128,3584]{1,0:T(8,128)(2,1)} %get-tuple-element.349), channel_id=1, source_target_pairs={{16,0},{32,16},{48,32},{64,48},{80,64},{96,80},{112,96},{17,1},{33... | collective-permute-start | bytes 2752520 | tf_op jit(solution)/shard_map/while/body/eval_jaxpr/ppermute | solution.py:11
  477.8 14.9 %collective-permute-start = (bf16[128,3584]{1,0:T(8,128)(2,1)}, bf16[128,3584]{1,0:T(8,128)(2,1)S(1)}, u32[]{:S(2)}, u32[]{:S(2)}) collective-permute-start(bf16[128,3584]{1,0:T(8,128)(2,1)} %get-tuple-element.349), channel_id=1, source_target_pairs={{16,0},{32,16},{48,32},{64,48},{80,64},{96,80},{112,96},{17,1},{33... | collective-permute-start | bytes 2752520 | tf_op jit(solution)/shard_map/while/body/eval_jaxpr/ppermute | solution.py:11
  497.6 14.9 %collective-permute-start = (bf16[128,3584]{1,0:T(8,128)(2,1)}, bf16[128,3584]{1,0:T(8,128)(2,1)S(1)}, u32[]{:S(2)}, u32[]{:S(2)}) collective-permute-start(bf16[128,3584]{1,0:T(8,128)(2,1)} %get-tuple-element.349), channel_id=1, source_target_pairs={{16,0},{32,16},{48,32},{64,48},{80,64},{96,80},{112,96},{17,1},{33... | collective-permute-start | bytes 2752520 | tf_op jit(solution)/shard_map/while/body/eval_jaxpr/ppermute | solution.py:11
  517.5 78.6 %collective-permute-start = (bf16[128,3584]{1,0:T(8,128)(2,1)}, bf16[128,3584]{1,0:T(8,128)(2,1)S(1)}, u32[]{:S(2)}, u32[]{:S(2)}) collective-permute-start(bf16[128,3584]{1,0:T(8,128)(2,1)} %get-tuple-element.349), channel_id=1, source_target_pairs={{16,0},{32,16},{48,32},{64,48},{80,64},{96,80},{112,96},{17,1},{33... | collective-permute-start | bytes 2752520 | tf_op jit(solution)/shard_map/while/body/eval_jaxpr/ppermute | solution.py:11
  615.1 14.8 %collective-permute-start = (bf16[128,3584]{1,0:T(8,128)(2,1)}, bf16[128,3584]{1,0:T(8,128)(2,1)S(1)}, u32[]{:S(2)}, u32[]{:S(2)}) collective-permute-start(bf16[128,3584]{1,0:T(8,128)(2,1)} %get-tuple-element.349), channel_id=1, source_target_pairs={{16,0},{32,16},{48,32},{64,48},{80,64},{96,80},{112,96},{17,1},{33... | collective-permute-start | bytes 2752520 | tf_op jit(solution)/shard_map/while/body/eval_jaxpr/ppermute | solution.py:11
  648.8 14.9 %collective-permute-start = (bf16[128,3584]{1,0:T(8,128)(2,1)}, bf16[128,3584]{1,0:T(8,128)(2,1)S(1)}, u32[]{:S(2)}, u32[]{:S(2)}) collective-permute-start(bf16[128,3584]{1,0:T(8,128)(2,1)} %get-tuple-element.349), channel_id=1, source_target_pairs={{16,0},{32,16},{48,32},{64,48},{80,64},{96,80},{112,96},{17,1},{33... | collective-permute-start | bytes 2752520 | tf_op jit(solution)/shard_map/while/body/eval_jaxpr/ppermute | solution.py:11
  682.7 14.9 %collective-permute-start = (bf16[128,3584]{1,0:T(8,128)(2,1)}, bf16[128,3584]{1,0:T(8,128)(2,1)S(1)}, u32[]{:S(2)}, u32[]{:S(2)}) collective-permute-start(bf16[128,3584]{1,0:T(8,128)(2,1)} %get-tuple-element.349), channel_id=1, source_target_pairs={{16,0},{32,16},{48,32},{64,48},{80,64},{96,80},{112,96},{17,1},{33... | collective-permute-start | bytes 2752520 | tf_op jit(solution)/shard_map/while/body/eval_jaxpr/ppermute | solution.py:11
  716.5 4.6 collective-permute-start
  746.1 15.3 %all-to-all-start.2 = ((f32[16,32,224]{2,1,0:T(8,128)}), f32[16,32,224]{2,1,0:T(8,128)S(1)}, u32[]{:S(2)}, u32[]{:S(2)}) async-start(f32[16,32,224]{2,1,0:T(8,128)} %copy.13), calls=%async_computation.2 | async-start | bytes 1048576 | tf_op jit(solution)/shard_map/all_to_all | solution.py:33
